TPU v7x, 32 devices: a whole 2x2x4 slice. The times are simulated.
32 devices in a mesh: fsdp: 8 (over z, y), rep: 4 (over x, core).
Axes of the slice: x: 2, y: 2, z: 4, core: 2. Of those that a mesh axis runs over, the one named last changes fastest.
Arguments:
- hidden: bfloat16 [8192, 2048], P(('fsdp', 'rep')), may hold values from -6 to 6
- attn_gain: bfloat16 [2048], P(('fsdp', 'rep')), may hold values from 0.25 to 1.75
- w_query: bfloat16 [2048, 2048], P(('fsdp', 'rep')), as said below
- w_key: bfloat16 [2048, 512], P(('fsdp', 'rep')), as said below
- w_value: bfloat16 [2048, 512], P(('fsdp', 'rep')), may hold values from -0.125 to 0.125
- w_out: bfloat16 [2048, 2048], P(None, ('fsdp', 'rep')), may hold values from -0.125 to 0.125
Outputs:
- mixed: bfloat16 [8192, 2048], P(('fsdp', 'rep'))
Inputs may be any that keep to these rules, and one draw needn't show every extreme that they name: `w_query`: entries of order 2048^(-1/2). `w_key`: entries of order 2048^(-1/2) times a factor up to twenty.
All inputs are finite; a program needn't handle non-finite values.
Results may differ from a plain program's by a relative error of at most 0.012.
The roundings to bfloat16 on the way count: a program that leaves them out, or rounds other values in their place, can miss the bound.
Values may be sent and summed in bfloat16 or wider, within the bound.
A program may use at most 64 MiB of HBM per device.

v0:
```python
import jax
import jax.numpy as jnp
from jax import lax
from jax.sharding import PartitionSpec as P

HD = 64


rope_base = 500000.0
norm_eps = 1e-05


def rope_tables(tokens, head_dim):
    position = jnp.arange(tokens, dtype=jnp.float32)
    freq = rope_base ** (-(jnp.arange(head_dim // 2, dtype=jnp.float32) * 2.0) / head_dim)
    angle = position[:, None] * freq[None, :]
    cos_table = jnp.concatenate([jnp.cos(angle), jnp.cos(angle)], axis=-1)
    sin_table = jnp.concatenate([jnp.sin(angle), jnp.sin(angle)], axis=-1)
    return (cos_table, sin_table)


def rotate(tensor, cos_table, sin_table):
    half = tensor.shape[-1] // 2
    turned = jnp.concatenate([-tensor[..., half:], tensor[..., :half]], axis=-1)
    return tensor * cos_table + turned * sin_table


def body(hidden, attn_gain, w_query, w_key, w_value, w_out):
    tokens = hidden.shape[0]
    head_dim = HD
    width_query = w_query.shape[1]
    width_kv = w_key.shape[1]
    kv_count = width_kv // head_dim
    group = width_query // width_kv
    x_float = hidden.astype(jnp.float32)
    inv_rms = lax.rsqrt(jnp.mean(x_float * x_float, axis=-1, keepdims=True) + norm_eps)
    gain_piece = lax.all_gather(attn_gain, ("fsdp", "rep"), axis=0, tiled=True)
    query_piece = lax.all_gather(w_query, ("fsdp", "rep"), axis=0, tiled=True)
    key_piece = lax.all_gather(w_key, ("fsdp", "rep"), axis=0, tiled=True)
    value_piece = lax.all_gather(w_value, ("fsdp", "rep"), axis=0, tiled=True)
    normed = (x_float * inv_rms * gain_piece.astype(jnp.float32)[None, :]).astype(jnp.bfloat16)
    queries = jnp.dot(normed, query_piece, preferred_element_type=jnp.float32)
    keys_raw = jnp.dot(normed, key_piece, preferred_element_type=jnp.float32)
    values_raw = jnp.dot(normed, value_piece, preferred_element_type=jnp.float32)
    cos_table, sin_table = rope_tables(tokens, head_dim)
    queries = queries.reshape(tokens, kv_count, group, head_dim)
    keys_raw = keys_raw.reshape(tokens, kv_count, head_dim)
    values_bf = values_raw.reshape(tokens, kv_count, head_dim).astype(jnp.bfloat16)
    rope_queries = rotate(queries, cos_table[:, None, None, :], sin_table[:, None, None, :]).astype(
        jnp.bfloat16
    )
    rope_keys = rotate(keys_raw, cos_table[:, None, :], sin_table[:, None, :]).astype(jnp.bfloat16)
    scores = jnp.einsum(
        "qkgd,skd->kgqs", rope_queries, rope_keys, preferred_element_type=jnp.float32
    ) * head_dim ** (-0.5)
    causal = jnp.arange(tokens)[:, None] >= jnp.arange(tokens)[None, :]
    scores = jnp.where(causal[None, None, :, :], scores, -1e30)
    top = jnp.max(scores, axis=-1, keepdims=True)
    expo = jnp.exp(scores - top)
    probs = (expo / jnp.sum(expo, axis=-1, keepdims=True)).astype(jnp.bfloat16)
    context = jnp.einsum("kgqs,skd->qkgd", probs, values_bf, preferred_element_type=jnp.float32)
    context = context.reshape(tokens, width_query).astype(jnp.bfloat16)
    branch = jnp.dot(
        context,
        lax.all_gather(w_out, ("fsdp", "rep"), axis=1, tiled=True),
        preferred_element_type=jnp.float32,
    )
    return (x_float + branch).astype(jnp.bfloat16)


def solution(mesh):
    placed = (
        P(("fsdp", "rep"), None),
        P(("fsdp", "rep")),
        P(("fsdp", "rep"), None),
        P(("fsdp", "rep"), None),
        P(("fsdp", "rep"), None),
        P(None, ("fsdp", "rep")),
    )
    return jax.shard_map(
        body, mesh=mesh, in_specs=placed, out_specs=P(("fsdp", "rep"), None), check_vma=False
    )
```

profile of v0, /device:TPU:0, one launch (start us, length us, event | category | flops | bytes accessed | tf_op | source)
XLA Modules:
  0.0 297.6 jit_solution(9203486270447136202)
XLA Ops:
  6.5 0.0 all-gather.5.cloned.1.call-start
  6.5 0.7 all-gather.5.cloned.1.call-update
  7.3 0.0 all-gather.7.cloned.1.call-start
  7.3 0.7 all-gather.7.cloned.1.call-update
  8.0 0.0 all-gather.9.cloned.1.call-start
  8.1 0.7 all-gather.9.cloned.1.call-update
  8.7 0.0 all-gather.11.cloned.1.call-start
  8.8 0.5 all-gather.11.cloned.1.call-update
  9.3 0.9 dynamic-update-slice
  10.2 42.0 %all-reduce = bf16[2048]{0:T(1024)(128)(2,1)S(1)} all-reduce(bf16[2048]{0:T(1024)(128)(2,1)S(1)} %dynamic-update-slice), channel_id=1, replica_groups=mesh['fsdp'=8,'rep'=4] {'fsdp','rep'}, use_global_device_ids=true, to_apply=%add | all-reduce | flops 2048 | bytes 8192
  52.3 0.2 fusion.24
  52.5 1.5 fusion.7
  54.0 0.0 copy-start
  54.0 15.2 %all-gather.5.cloned.1.call-done = bf16[2048,512]{1,0:T(8,128)(2,1)} async-done(((bf16[64,512]{1,0:T(8,128)(2,1)}), bf16[2048,512]{1,0:T(8,128)(2,1)}) %all-gather.5.cloned.1.call-update) | async-done | bytes 2097168 | tf_op jit(solution)/shard_map/all_gather | solution.py:40
  69.2 2.7 convolution_convert_fusion
  71.8 0.1 copy.15
  72.0 55.1 %all-gather.7.cloned.1.call-done = bf16[2048,512]{1,0:T(8,128)(2,1)} async-done(((bf16[64,512]{1,0:T(8,128)(2,1)}), bf16[2048,512]{1,0:T(8,128)(2,1)}) %all-gather.7.cloned.1.call-update) | async-done | bytes 2097168 | tf_op jit(solution)/shard_map/all_gather | solution.py:39
  127.1 0.0 copy-done
  127.1 2.6 fusion.30
  129.8 76.1 %all-gather.9.cloned.1.call-done = bf16[2048,2048]{1,0:T(8,128)(2,1)} async-done(((bf16[64,2048]{1,0:T(8,128)(2,1)}), bf16[2048,2048]{1,0:T(8,128)(2,1)}) %all-gather.9.cloned.1.call-update) | async-done | bytes 8388624 | tf_op jit(solution)/shard_map/all_gather | solution.py:38
  205.9 6.8 %fusion.28 = f32[256,2048]{0,1:T(8,128)S(1)} fusion(bf16[2048,2048]{1,0:T(8,128)(2,1)} %all-gather.9.cloned.1.call-done, bf16[256,2048]{1,0:T(8,128)(2,1)S(1)} %copy-done, f32[2048]{0:T(1024)S(1)} %convert_element_type.37, f32[256]{0:T(256)S(1)} %add_rsqrt_fusion), kind=kOutput, calls=%fused_computation.43 | convolution fusion | flops 2149580800 | bytes 11543552 | tf_op jit(solution)/shard_map/dot_general | solution.py:42
  212.7 0.2 slice_negate_fusion
  212.9 1.3 fusion.13
  214.2 2.5 fusion.33
  216.7 0.9 fusion.12
  217.6 66.7 %all-gather.11.cloned.1.call-done = bf16[2048,2048]{0,1:T(8,128)(2,1)} async-done(((bf16[2048,64]{0,1:T(8,128)(2,1)}), bf16[2048,2048]{0,1:T(8,128)(2,1)}) %all-gather.11.cloned.1.call-update) | async-done | bytes 8388624 | tf_op jit(solution)/shard_map/all_gather | solution.py:65
  284.3 6.7 %fusion.6 = bf16[256,2048]{1,0:T(8,128)(2,1)} fusion(bf16[256,2048]{0,1:T(8,128)(2,1)S(1)} %bitcast.37, bf16[2048,2048]{0,1:T(8,128)(2,1)} %all-gather.11.cloned.1.call-done, bf16[256,2048]{1,0:T(8,128)(2,1)S(1)} %copy-done), kind=kOutput, calls=%fused_computation.12 | convolution fusion | flops 2149056512 | bytes 11534336 | tf_op jit(solution)/shard_map/dot_general | solution.py:63
  (7 shorter events, 0.1 us)
Async XLA Ops:
  6.5 62.6 %all-gather.5.cloned.1.call-start = ((), (), s32[]{:S(2)}) async-start(), calls=%async_computation | async-start | bytes 2162688 | tf_op jit(solution)/shard_map/all_gather | solution.py:40
  7.3 119.8 %all-gather.7.cloned.1.call-start = ((), (), s32[]{:S(2)}) async-start(), calls=%async_computation.1 | async-start | bytes 2162688 | tf_op jit(solution)/shard_map/all_gather | solution.py:39
  8.0 197.9 %all-gather.9.cloned.1.call-start = ((), (), s32[]{:S(2)}) async-start(), calls=%async_computation.2 | async-start | bytes 8650752 | tf_op jit(solution)/shard_map/all_gather | solution.py:38
  8.7 275.6 %all-gather.11.cloned.1.call-start = ((), (), s32[]{:S(2)}) async-start(), calls=%async_computation.3 | async-start | bytes 8650752 | tf_op jit(solution)/shard_map/all_gather | solution.py:65
  54.0 73.1 %copy-start = (bf16[256,2048]{1,0:T(8,128)(2,1)S(1)}, bf16[256,2048]{1,0:T(8,128)(2,1)}, u32[]{:S(2)}) copy-start(bf16[256,2048]{1,0:T(8,128)(2,1)} %param.6) | copy-start | bytes 3145732
Sparse Core Ops, SparseCore 0:
  10.2 58.9 all-gather.4
  72.0 55.0 all-gather.6
  130.0 75.8 all-gather.8
  208.6 75.6 all-gather.10
where the time goes:
time: 298 us
  waiting for transfers between devices  216 us (72%)
  blocking collectives  42 us (14%)
  matrix products  21.1 us (7%)
  between operations  13.2 us (4%)
  other arithmetic  4.44 us (1%)
    all_gather x1, waiting for transfers between devices, body(): query_piece = lax.all_gather(w_query, ('fsdp', 'rep'), axis=0, tiled=True)  76.1 us
    all_gather x1, waiting for transfers between devices, body(): lax.all_gather(w_out, ('fsdp', 'rep'), axis=1, tiled=True)  66.7 us
    all_gather x1, waiting for transfers between devices, body(): key_piece = lax.all_gather(w_key, ('fsdp', 'rep'), axis=0, tiled=True)  55.1 us
    unnamed x1, blocking collectives  42 us
    all_gather x1, waiting for transfers between devices, body(): value_piece = lax.all_gather(w_value, ('fsdp', 'rep'), axis=0, tiled=True)  15.2 us
    dot_general x1, matrix products, body(): queries = jnp.dot(normed, query_piece, preferred_element_type=jnp.float32)  6.84 us
    dot_general x1, matrix products, body(): jnp.dot(context, lax.all_gather(w_out, ('fsdp', 'rep'), axis=1, tiled=Tru...  6.74 us
  transfers between devices with their start and end apart: 4, of which 4 were waited for; matrix products, arithmetic and copies ran while one was open for 7% of the time, Pallas kernels for 0%

commit v1 on v0

--- a/solution.py
+++ b/solution.py
@@ -34,10 +34,21 @@
     group = width_query // width_kv
     x_float = hidden.astype(jnp.float32)
     inv_rms = lax.rsqrt(jnp.mean(x_float * x_float, axis=-1, keepdims=True) + norm_eps)
-    gain_piece = lax.all_gather(attn_gain, ("fsdp", "rep"), axis=0, tiled=True)
-    query_piece = lax.all_gather(w_query, ("fsdp", "rep"), axis=0, tiled=True)
-    key_piece = lax.all_gather(w_key, ("fsdp", "rep"), axis=0, tiled=True)
-    value_piece = lax.all_gather(w_value, ("fsdp", "rep"), axis=0, tiled=True)
+    width_rows = w_query.shape[0]
+    packed = jnp.concatenate(
+        [w_query, w_key, w_value, w_out.T, jnp.broadcast_to(attn_gain[:, None], (width_rows, 128))],
+        axis=1,
+    )
+    packed = lax.all_gather(packed, ("fsdp", "rep"), axis=0, tiled=True)
+    cut_key = width_query
+    cut_value = cut_key + width_kv
+    cut_out = cut_value + width_kv
+    cut_gain = cut_out + w_out.shape[0]
+    query_piece = packed[:, :cut_key]
+    key_piece = packed[:, cut_key:cut_value]
+    value_piece = packed[:, cut_value:cut_out]
+    out_piece = packed[:, cut_out:cut_gain]
+    gain_piece = packed[:, cut_gain]
     normed = (x_float * inv_rms * gain_piece.astype(jnp.float32)[None, :]).astype(jnp.bfloat16)
     queries = jnp.dot(normed, query_piece, preferred_element_type=jnp.float32)
     keys_raw = jnp.dot(normed, key_piece, preferred_element_type=jnp.float32)
@@ -60,10 +71,8 @@
     probs = (expo / jnp.sum(expo, axis=-1, keepdims=True)).astype(jnp.bfloat16)
     context = jnp.einsum("kgqs,skd->qkgd", probs, values_bf, preferred_element_type=jnp.float32)
     context = context.reshape(tokens, width_query).astype(jnp.bfloat16)
-    branch = jnp.dot(
-        context,
-        lax.all_gather(w_out, ("fsdp", "rep"), axis=1, tiled=True),
-        preferred_element_type=jnp.float32,
+    branch = lax.dot_general(
+        context, out_piece, (((1,), (1,)), ((), ())), preferred_element_type=jnp.float32
     )
     return (x_float + branch).astype(jnp.bfloat16)
 

time: 298 us -> 190 us (0.64)
  waiting for transfers between devices: 216 us -> 138 us
  blocking collectives: 42 us -> 0 us
  local copies, waits for them, and re-layouts: 1 us -> 8.45 us
    all_gather x4 -> x1, waiting for transfers between devices: 213 us -> 138 us  [body(): packed = lax.all_gather(packed, ('fsdp', 'rep'), axis=0, tiled=True)]
    unnamed x1 -> x0, blocking collectives: 42 us -> none
    unnamed x4 -> x18, local copies, waits for them, and re-layouts: 0.87 us -> 5.93 us
  transfers between devices with their start and end apart: 4 -> 1, of which waited for: 4 -> 1; matrix products, arithmetic and copies ran while one was open for 7% -> 1% of each run, Pallas kernels for 0% -> 0%
where the time goes in v1:
time: 190 us
  waiting for transfers between devices  138 us (73%)
  matrix products  22.9 us (12%)
  between operations  13.5 us (7%)
  local copies, waits for them, and re-layouts  8.45 us (4%)
  other arithmetic  6.64 us (3%)
    all_gather x1, waiting for transfers between devices, body(): packed = lax.all_gather(packed, ('fsdp', 'rep'), axis=0, tiled=True)  138 us
    dot_general x1, matrix products, body(): queries = jnp.dot(normed, query_piece, preferred_element_type=jnp.float32)  6.84 us
    dot_general x1, matrix products, body(): lax.dot_general(context, out_piece, (((1,), (1,)), ((), ())), preferred_e...  6.74 us
    unnamed x18, local copies, waits for them, and re-layouts  5.93 us
  transfers between devices with their start and end apart: 1, of which 1 were waited for; matrix products, arithmetic and copies ran while one was open for 1% of the time, Pallas kernels for 0%

profile of v1, /device:TPU:0, one launch (start us, length us, event | category | flops | bytes accessed | tf_op | source)
XLA Modules:
  0.0 189.6 jit_solution(6654634190219284311)
XLA Ops:
  6.5 0.0 all-gather.2.cloned.1.call-start
  6.5 1.1 constant_dynamic-update-slice_fusion.3
  7.6 0.8 constant_dynamic-update-slice_fusion.2
  8.4 0.8 constant_dynamic-update-slice_fusion.1
  9.3 1.0 bitcast_dynamic-update-slice_fusion
  10.3 0.7 constant_dynamic-update-slice_fusion
  11.0 0.0 copy-start.1
  11.0 0.8 copy-done.1
  11.8 0.0 all-gather.2.cloned.1.call-update
  11.9 0.6 iota_compare_fusion
  12.5 0.2 fusion.39
  12.7 0.0 copy-done.2
  12.8 0.3 fusion.15
  13.1 138.0 %all-gather.2.cloned.1.call-done = bf16[2048,5248]{1,0:T(8,128)(2,1)} async-done(((bf16[64,5248]{1,0:T(8,128)(2,1)}), bf16[2048,5248]{1,0:T(8,128)(2,1)}) %all-gather.2.cloned.1.call-update) | async-done | bytes 21495824 | tf_op jit(solution)/shard_map/all_gather | solution.py:42
  151.1 1.3 convert_reduce_fusion
  152.3 6.8 %fusion.3 = f32[256,2048]{0,1:T(8,128)S(1)} fusion(bf16[2048,5248]{1,0:T(8,128)(2,1)} %all-gather.2.cloned.1.call-done, bf16[256,2048]{1,0:T(8,128)(2,1)S(1)} %copy-done.2, f32[2048]{0:T(1024)S(1)} %convert_reduce_fusion, f32[256]{0:T(256)S(1)} %add_rsqrt_fusion), kind=kOutput, calls=%fused_computation.3 | convolution fusion | flops 2149580800 | bytes 11543552 | tf_op jit(solution)/shard_map/dot_general | solution.py:53
  159.2 0.0 copy-start.3
  159.2 1.2 slice_negate_fusion
  160.4 0.2 copy-done.3
  160.6 2.6 %fusion.18 = f32[256,512]{0,1:T(8,128)S(1)} fusion(bf16[2048,5248]{1,0:T(8,128)(2,1)} %all-gather.2.cloned.1.call-done, bf16[256,2048]{1,0:T(8,128)(2,1)S(1)} %copy-done.3, f32[2048]{0:T(1024)S(1)} %convert_reduce_fusion, f32[256]{0:T(256)S(1)} %add_rsqrt_fusion), kind=kOutput, calls=%fused_computation.20 | convolution fusion | flops 538968064 | bytes 3679232 | tf_op jit(solution)/shard_map/dot_general | solution.py:54
  163.2 0.0 copy-start
  163.3 0.8 copy-done
  164.1 0.8 slice_negate_fusion.1
  164.8 3.1 %fusion.25 = bf16[256,512]{1,0:T(8,128)(2,1)} fusion(bf16[2048,5248]{1,0:T(8,128)(2,1)} %all-gather.2.cloned.1.call-done, bf16[256,2048]{1,0:T(8,128)(2,1)S(1)} %copy-done.3, f32[2048]{0:T(1024)S(1)} %convert_reduce_fusion, f32[256]{0:T(256)S(1)} %add_rsqrt_fusion), kind=kOutput, calls=%fused_computation.28 | convolution fusion | flops 539099136 | bytes 3417088 | tf_op jit(solution)/shard_map/dot_general | solution.py:55
  167.9 1.8 copy.15
  169.7 2.8 %fusion.28 = f32[8,256,256,4]{2,1,3,0:T(8,128)S(1)} fusion(f32[256,8,4,32]{0,3,2,1:T(8,128)} %get-tuple-element.6, f32[256,8,4,32]{0,3,2,1:T(8,128)S(1)} %get-tuple-element.5, f32[256,8,4,64]{0,3,2,1:T(8,128)S(1)} %bitcast.31, f32[256,64]{0,1:T(8,128)S(1)} %get-tuple-element.14, f32[256,64]{0,1:T(8,128)S(1)} %get-tuple-element.13, ...), kind=kOutput, calls=%fused_computation.29 | convolution fusion | flops 271712256 | bytes 13762560 | tf_op jit(solution)/shard_map/qkgd,skd->kgqs/dot_general | solution.py:64
  172.5 0.0 copy-done.6
  172.5 2.3 %fusion.46 = (f32[8,4,256]{2,1,0:T(4,128)S(1)}, f32[8,4,256,256]{2,3,1,0:T(8,128)S(1)}) fusion(f32[8,256,256,4]{2,1,3,0:T(8,128)S(1)} %fusion.28, pred[256,256]{0,1:T(8,128)(4,1)S(1)} %copy-done.6), kind=kOutput, calls=%fused_computation.57 | output fusion | flops 12583167 | bytes 16875520 | tf_op jit(solution)/shard_map/sub | solution.py:70
  174.8 0.0 copy-start.4
  174.8 0.9 fusion.24
  175.7 0.4 copy-done.4
  176.0 6.7 %fusion.12 = bf16[256,2048]{1,0:T(8,128)(2,1)} fusion(bf16[256,2048]{0,1:T(8,128)(2,1)S(1)} %bitcast.35, bf16[2048,5248]{1,0:T(8,128)(2,1)} %all-gather.2.cloned.1.call-done, bf16[256,2048]{1,0:T(8,128)(2,1)S(1)} %copy-done.4), kind=kOutput, calls=%fused_computation.16 | convolution fusion | flops 2149056512 | bytes 11534336 | tf_op jit(solution)/shard_map/dot_general | solution.py:74
  (7 shorter events, 0.0 us)
Async XLA Ops:
  6.5 6.2 %copy-start.2 = (bf16[256,2048]{1,0:T(8,128)(2,1)S(1)}, bf16[256,2048]{1,0:T(8,128)(2,1)}, u32[]{:S(2)}) copy-start(bf16[256,2048]{1,0:T(8,128)(2,1)} %param.6) | copy-start | bytes 3145732
  6.5 144.6 %all-gather.2.cloned.1.call-start = ((), (), s32[]{:S(2)}) async-start(), calls=%async_computation | async-start | bytes 22167552 | tf_op jit(solution)/shard_map/all_gather | solution.py:42
  11.0 0.8 copy-start.1
  159.2 1.4 copy-start.3
  163.2 0.8 copy-start
  169.7 2.8 %copy-start.6 = (pred[256,256]{0,1:T(8,128)(4,1)S(1)}, pred[256,256]{0,1:T(8,128)(4,1)}, u32[]{:S(2)}) copy-start(pred[256,256]{0,1:T(8,128)(4,1)} %iota_compare_fusion) | copy-start | bytes 196612
  172.5 2.3 %copy-start.5 = (bf16[256,512]{0,1:T(8,128)(2,1)S(1)}, bf16[256,512]{0,1:T(8,128)(2,1)}, u32[]{:S(2)}) copy-start(bf16[256,512]{0,1:T(8,128)(2,1)} %copy.15) | copy-start | bytes 786436
  174.8 1.2 copy-start.4
Sparse Core Ops, SparseCore 0:
  12.0 139.0 all-gather.1

commit v2 on v1

--- a/solution.py
+++ b/solution.py
@@ -1,6 +1,10 @@
+import functools
+
 import jax
 import jax.numpy as jnp
 from jax import lax
+from jax.experimental import pallas as pl
+from jax.experimental.pallas import tpu as pltpu
 from jax.sharding import PartitionSpec as P
 
 HD = 64
@@ -25,7 +29,168 @@
     return tensor * cos_table + turned * sin_table
 
 
-def body(hidden, attn_gain, w_query, w_key, w_value, w_out):
+ORDERS = ((("x", "z", "y"), 2), (("y", "z", "x"), 2), (("z", "x", "y"), 1), (("z", "y", "x"), 1))
+KERNEL_DEVICES = 64
+
+
+def chip_grid(fsdp, rep):
+    x_count = max(rep // 2, 1)
+    return {"z": fsdp // x_count, "y": x_count, "x": x_count}
+
+
+def column_parts(width):
+    tiles = width // 128
+    total = sum(weight for _, weight in ORDERS)
+    cuts, seen = [0], 0
+    for _, weight in ORDERS:
+        seen += weight
+        cuts.append((tiles * seen + total // 2) // total * 128)
+    return [(order, cuts[i], cuts[i + 1] - cuts[i]) for i, (order, _) in enumerate(ORDERS)]
+
+
+def gather_kernel(fsdp, rep, shard, out, send_sem, recv_sem, own_sem):
+    grid = chip_grid(fsdp, rep)
+    row, col = lax.axis_index("fsdp"), lax.axis_index("rep")
+    here = {"z": row // grid["y"], "y": row % grid["y"], "x": col // 2}
+    core = col % 2
+    parts = column_parts(shard.shape[1])
+    chips = fsdp * rep // 2
+
+    def device(at, which):
+        return (at["z"] * grid["y"] + at["y"], at["x"] * 2 + which)
+
+    def slot_of(at, which):
+        place = device(at, which)
+        return place[0] * rep + place[1]
+
+    def nearest(dim, step):
+        p, n = here[dim], grid[dim]
+        if n != 4:
+            return (p + step) % n
+        middle = jnp.where((p == 1) | (p == 2), 1, 0)
+        high = step // 2
+        low = step % 2
+        low = low + middle * high * (1 - 2 * low)
+        first = (1 - 2 * (p % 2)) * low
+        return p + first + (2 - 4 * (p // 2)) * high
+
+    def origin(step):
+        return {
+            "z": nearest("z", step // (grid["y"] * grid["x"])),
+            "y": nearest("y", (step // grid["x"]) % grid["y"]),
+            "x": nearest("x", step % grid["x"]),
+        }
+
+    def steps_along(dim, start):
+        p, n = here[dim], grid[dim]
+        if n == 2:
+            return [(1 - p, p == start)]
+        return [(p + 1, (p >= start) & (p + 1 < n)), (p - 1, (p <= start) & (p >= 1))]
+
+    def moves(order, at):
+        found = []
+        for i, dim in enumerate(order):
+            for target, go in steps_along(dim, at[dim]):
+                for later in order[i + 1 :]:
+                    go = go & (here[later] == at[later])
+                found.append((go, device({**here, dim: target}, core)))
+        found.append((None, device(here, 1 - core)))
+        return found
+
+    def copy(source, slot, step, part, move, target):
+        _, begin, size = parts[part]
+        piece = source if source is shard else out.at[slot]
+        return pltpu.make_async_remote_copy(
+            src_ref=piece.at[:, pl.ds(begin, size)],
+            dst_ref=out.at[slot, :, pl.ds(begin, size)],
+            send_sem=send_sem.at[step, part, move],
+            recv_sem=recv_sem.at[slot, part],
+            device_id=target,
+            device_id_type=pl.DeviceIdType.MESH,
+        )
+
+    def each_move(source, step, part, act):
+        at = origin(step)
+        slot = slot_of(at, core)
+        for move, (go, target) in enumerate(moves(parts[part][0], at)):
+            if go is None:
+                act(copy(source, slot, step, part, move, target))
+            else:
+
+                @pl.when(go)
+                def _(move=move, target=target):
+                    act(copy(source, slot, step, part, move, target))
+
+    barrier = pltpu.get_barrier_semaphore()
+    around = [(None, device(here, 1 - core))]
+    for dim in ("z", "y", "x"):
+        for target, go in steps_along(dim, here[dim]):
+            around.append((go, device({**here, dim: target}, core)))
+    count = 0
+    for go, target in around:
+        if go is None:
+            pl.semaphore_signal(
+                barrier, inc=1, device_id=target, device_id_type=pl.DeviceIdType.MESH
+            )
+            count = count + 1
+        else:
+
+            @pl.when(go)
+            def _(target=target):
+                pl.semaphore_signal(
+                    barrier, inc=1, device_id=target, device_id_type=pl.DeviceIdType.MESH
+                )
+
+            count = count + jnp.where(go, 1, 0)
+    pl.semaphore_wait(barrier, count)
+
+    own = pltpu.make_async_copy(shard, out.at[slot_of(here, core)], own_sem)
+    for part in range(len(parts)):
+        each_move(shard, 0, part, lambda c: c.start())
+    own.start()
+
+    def forward(step, carry):
+        at = origin(step)
+        for part in range(len(parts)):
+            copy(out, slot_of(at, core), step, part, 0, device(here, 1 - core)).wait_recv()
+            each_move(out, step, part, lambda c: c.start())
+        return carry
+
+    lax.fori_loop(1, chips, forward, 0)
+    own.wait()
+
+    def finish(step, carry):
+        at = origin(step)
+        for part in range(len(parts)):
+            copy(out, slot_of(at, 1 - core), step, part, 0, device(here, 1 - core)).wait_recv()
+            each_move(out, step, part, lambda c: c.wait_send())
+        return carry
+
+    lax.fori_loop(0, chips, finish, 0)
+
+
+def gather_rows(shard, fsdp, rep):
+    rows, width = shard.shape
+    grid = chip_grid(fsdp, rep)
+    moves = 1 + sum(1 if n == 2 else 2 for n in grid.values())
+    devices = fsdp * rep
+    gathered = pl.pallas_call(
+        functools.partial(gather_kernel, fsdp, rep),
+        out_shape=jax.ShapeDtypeStruct((devices, rows, width), shard.dtype),
+        in_specs=[pl.BlockSpec(memory_space=pltpu.VMEM)],
+        out_specs=pl.BlockSpec(memory_space=pl.ANY),
+        scratch_shapes=[
+            pltpu.SemaphoreType.DMA((devices // 2, len(ORDERS), moves)),
+            pltpu.SemaphoreType.DMA((devices, len(ORDERS))),
+            pltpu.SemaphoreType.DMA,
+        ],
+        compiler_params=pltpu.CompilerParams(collective_id=0, has_side_effects=True),
+        name="gather_rows",
+    )(shard)
+    return gathered.reshape(devices * rows, width)
+
+
+def body(fsdp, rep, hidden, attn_gain, w_query, w_key, w_value, w_out):
     tokens = hidden.shape[0]
     head_dim = HD
     width_query = w_query.shape[1]
@@ -39,7 +204,11 @@
         [w_query, w_key, w_value, w_out.T, jnp.broadcast_to(attn_gain[:, None], (width_rows, 128))],
         axis=1,
     )
-    packed = lax.all_gather(packed, ("fsdp", "rep"), axis=0, tiled=True)
+    x_count = rep // 2
+    if rep % 2 == 0 and x_count > 1 and fsdp % x_count == 0 and fsdp * rep <= KERNEL_DEVICES:
+        packed = gather_rows(packed, fsdp, rep)
+    else:
+        packed = lax.all_gather(packed, ("fsdp", "rep"), axis=0, tiled=True)
     cut_key = width_query
     cut_value = cut_key + width_kv
     cut_out = cut_value + width_kv
@@ -87,5 +256,9 @@
         P(None, ("fsdp", "rep")),
     )
     return jax.shard_map(
-        body, mesh=mesh, in_specs=placed, out_specs=P(("fsdp", "rep"), None), check_vma=False
-    )
+        functools.partial(body, mesh.shape["fsdp"], mesh.shape["rep"]),
+        mesh=mesh,
+        in_specs=placed,
+        out_specs=P(("fsdp", "rep"), None),
+        check_vma=False,
+    )

time: 190 us -> 144 us (0.76)
  waiting for transfers between devices: 138 us -> 0 us
  Pallas kernels: 0 us -> 107 us
  between operations: 13.5 us -> 0.13 us
  local copies, waits for them, and re-layouts: 8.45 us -> 5.67 us
    all_gather x1 -> x0, waiting for transfers between devices: 138 us -> none  [body(): packed = lax.all_gather(packed, ('fsdp', 'rep'), axis=0, tiled=True)]
    pallas_call x0 -> x1, Pallas kernels: none -> 107 us  [gather_rows(): pl.pallas_call(functools.partial(gather_kernel, fsdp, rep), out_shape=jax...]
    dot_general x1, matrix products: 0.85 us -> 4.26 us  [body(): jnp.einsum('kgqs,skd->qkgd', probs, values_bf, preferred_element_type=jnp...]
    sub x1, other arithmetic: 2.27 us -> 4.57 us  [body(): expo = jnp.exp(scores - top)]
    unnamed x18 -> x9, local copies, waits for them, and re-layouts: 5.93 us -> 4.8 us
  transfers between devices with their start and end apart: 1 -> 0, of which waited for: 1 -> 0; matrix products, arithmetic and copies ran while one was open for 1% -> 0% of each run, Pallas kernels for 0% -> 0%
where the time goes in v2:
time: 144 us
  Pallas kernels  107 us (74%)
  matrix products  24.4 us (17%)
  other arithmetic  6.53 us (5%)
  local copies, waits for them, and re-layouts  5.67 us (4%)
    pallas_call x1, Pallas kernels, gather_rows(): pl.pallas_call(functools.partial(gather_kernel, fsdp, rep), out_shape=jax...  107 us
    dot_general x1, matrix products, body(): queries = jnp.dot(normed, query_piece, preferred_element_type=jnp.float32)  7.03 us
    dot_general x1, matrix products, body(): lax.dot_general(context, out_piece, (((1,), (1,)), ((), ())), preferred_e...  6.81 us
    unnamed x9, local copies, waits for them, and re-layouts  4.8 us
    sub x1, other arithmetic, body(): expo = jnp.exp(scores - top)  4.57 us
    dot_general x1, matrix products, body(): jnp.einsum('kgqs,skd->qkgd', probs, values_bf, preferred_element_type=jnp...  4.26 us

profile of v2, /device:TPU:0, one launch (start us, length us, event | category | flops | bytes accessed | tf_op | source)
XLA Modules:
  0.0 143.8 jit_solution(5411421366082495424)
XLA Ops:
  0.0 1.0 constant_dynamic-update-slice_fusion.3
  1.0 0.8 constant_dynamic-update-slice_fusion.2
  1.8 0.8 constant_dynamic-update-slice_fusion.1
  2.7 1.0 bitcast_dynamic-update-slice_fusion
  3.6 0.7 constant_dynamic-update-slice_fusion.shard
  4.4 0.0 copy-start
  4.4 0.8 copy-done
  5.2 107.2 %gather_rows.1 = bf16[32,64,5248]{2,1,0:T(8,128)(2,1)} custom-call(bf16[64,5248]{1,0:T(8,128)(2,1)} %copy-done), custom_call_target="tpu_custom_call" | custom-call | tf_op jit(solution)/shard_map/gather_rows/pallas_call | solution.py:177
  112.4 0.0 copy-start.1
  112.4 1.2 slice_convert_fusion
  113.6 0.3 copy.26
  113.9 0.0 copy-done.1
  113.9 0.3 fusion.15
  114.2 2.6 %fusion.18 = f32[256,512]{0,1:T(8,128)S(1)} fusion(bf16[2048,5248]{1,0:T(8,128)(2,1)} %bitcast.33, bf16[256,2048]{1,0:T(8,128)(2,1)S(1)} %copy-done.1, f32[2048]{0:T(1024)S(1)} %bitcast.42, f32[256]{0:T(256)S(1)} %add_rsqrt_fusion), kind=kOutput, calls=%fused_computation.20 | convolution fusion | flops 538968064 | bytes 3679232 | tf_op jit(solution)/shard_map/dot_general | solution.py:223
  116.9 7.0 %fusion.3 = f32[256,2048]{0,1:T(8,128)S(1)} fusion(bf16[2048,5248]{1,0:T(8,128)(2,1)} %bitcast.34, bf16[256,2048]{1,0:T(8,128)(2,1)S(1)} %copy-done.1, f32[2048]{0:T(1024)S(1)} %bitcast.43, f32[256]{0:T(256)S(1)} %add_rsqrt_fusion), kind=kOutput, calls=%fused_computation.3 | convolution fusion | flops 2149580800 | bytes 11543552 | tf_op jit(solution)/shard_map/dot_general | solution.py:222
  123.9 0.2 slice_negate_fusion
  124.1 0.2 fusion.39
  124.4 1.3 fusion.28
  125.7 4.6 %fusion.46 = (f32[8,4,256]{2,1,0:T(4,128)S(1)}, f32[8,4,256,256]{2,3,1,0:T(8,128)}) fusion(f32[8,256,256,4]{2,1,3,0:T(8,128)S(1)} %fusion.28, pred[256,256]{0,1:T(8,128)(4,1)S(1)} %iota_compare_fusion), kind=kOutput, calls=%fused_computation.57 | output fusion | flops 12583167 | bytes 16875520 | tf_op jit(solution)/shard_map/sub | solution.py:239
  130.3 2.3 %fusion.25 = bf16[256,512]{1,0:T(8,128)(2,1)S(1)} fusion(bf16[2048,5248]{1,0:T(8,128)(2,1)} %bitcast.35, bf16[256,2048]{1,0:T(8,128)(2,1)S(1)} %copy-done.1, f32[2048]{0:T(1024)S(1)} %bitcast.44, f32[256]{0:T(256)S(1)} %add_rsqrt_fusion), kind=kOutput, calls=%fused_computation.28 | convolution fusion | flops 539099136 | bytes 3417088 | tf_op jit(solution)/shard_map/dot_general | solution.py:224
  132.6 0.1 copy.16
  132.8 4.3 %fusion.24 = bf16[8,64,4,256]{3,1,2,0:T(8,128)(2,1)S(1)} fusion(bf16[256,8,64,1]{0,2,3,1:T(8,128)(2,1)S(1)} %bitcast.41, f32[8,4,256,256]{2,3,1,0:T(8,128)} %get-tuple-element.12, f32[8,4,256]{2,1,0:T(4,128)S(1)} %get-tuple-element.11), kind=kOutput, calls=%fused_computation.27 | convolution fusion | flops 273154048 | bytes 9732096 | tf_op jit(solution)/shard_map/kgqs,skd->qkgd/dot_general | solution.py:241
  137.0 6.8 %fusion.12 = bf16[256,2048]{1,0:T(8,128)(2,1)} fusion(bf16[256,2048]{0,1:T(8,128)(2,1)S(1)} %bitcast.45, bf16[2048,5248]{1,0:T(8,128)(2,1)} %bitcast.36, bf16[256,2048]{1,0:T(8,128)(2,1)S(1)} %copy-done.1), kind=kOutput, calls=%fused_computation.16 | convolution fusion | flops 2149056512 | bytes 11534336 | tf_op jit(solution)/shard_map/dot_general | solution.py:243
  (5 shorter events, 0.1 us)
Async XLA Ops:
  4.4 0.8 copy-start
  112.4 1.5 %copy-start.1 = (bf16[256,2048]{1,0:T(8,128)(2,1)S(1)}, bf16[256,2048]{1,0:T(8,128)(2,1)}, u32[]{:S(2)}) copy-start(bf16[256,2048]{1,0:T(8,128)(2,1)} %param.6) | copy-start | bytes 3145732

commit v3 on v2

--- a/solution.py
+++ b/solution.py
@@ -74,12 +74,12 @@
         first = (1 - 2 * (p % 2)) * low
         return p + first + (2 - 4 * (p // 2)) * high
 
-    def origin(step):
-        return {
-            "z": nearest("z", step // (grid["y"] * grid["x"])),
-            "y": nearest("y", (step // grid["x"]) % grid["y"]),
-            "x": nearest("x", step % grid["x"]),
-        }
+    def origin(step, order):
+        found = {}
+        for dim in order:
+            found[dim] = nearest(dim, step % grid[dim])
+            step = step // grid[dim]
+        return found
 
     def steps_along(dim, start):
         p, n = here[dim], grid[dim]
@@ -110,7 +110,7 @@
         )
 
     def each_move(source, step, part, act):
-        at = origin(step)
+        at = origin(step, parts[part][0])
         slot = slot_of(at, core)
         for move, (go, target) in enumerate(moves(parts[part][0], at)):
             if go is None:
@@ -150,8 +150,8 @@
     own.start()
 
     def forward(step, carry):
-        at = origin(step)
         for part in range(len(parts)):
+            at = origin(step, parts[part][0])
             copy(out, slot_of(at, core), step, part, 0, device(here, 1 - core)).wait_recv()
             each_move(out, step, part, lambda c: c.start())
         return carry
@@ -160,8 +160,8 @@
     own.wait()
 
     def finish(step, carry):
-        at = origin(step)
         for part in range(len(parts)):
+            at = origin(step, parts[part][0])
             copy(out, slot_of(at, 1 - core), step, part, 0, device(here, 1 - core)).wait_recv()
             each_move(out, step, part, lambda c: c.wait_send())
         return carry

time: 144 us -> 130 us (0.903)
  Pallas kernels: 107 us -> 92.4 us
    pallas_call x1, Pallas kernels: 107 us -> 92.4 us  [gather_rows(): pl.pallas_call(functools.partial(gather_kernel, fsdp, rep), out_shape=jax...]
where the time goes in v3:
time: 130 us; the launch traced here: 129 us
  Pallas kernels  92.4 us (71%)
  matrix products  24.4 us (19%)
  other arithmetic  6.53 us (5%)
  local copies, waits for them, and re-layouts  5.67 us (4%)
    pallas_call x1, Pallas kernels, gather_rows(): pl.pallas_call(functools.partial(gather_kernel, fsdp, rep), out_shape=jax...  92.4 us
    dot_general x1, matrix products, body(): queries = jnp.dot(normed, query_piece, preferred_element_type=jnp.float32)  7.03 us
    dot_general x1, matrix products, body(): lax.dot_general(context, out_piece, (((1,), (1,)), ((), ())), preferred_e...  6.81 us
    unnamed x9, local copies, waits for them, and re-layouts  4.8 us
    sub x1, other arithmetic, body(): expo = jnp.exp(scores - top)  4.57 us
    dot_general x1, matrix products, body(): jnp.einsum('kgqs,skd->qkgd', probs, values_bf, preferred_element_type=jnp...  4.26 us
    dot_general x1, matrix products, body(): keys_raw = jnp.dot(normed, key_piece, preferred_element_type=jnp.float32)  2.61 us

profile of v3, /device:TPU:0, one launch (start us, length us, event | category | flops | bytes accessed | tf_op | source)
XLA Modules:
  0.0 129.1 jit_solution(567840886937116323)
XLA Ops:
  0.0 1.0 constant_dynamic-update-slice_fusion.3
  1.0 0.8 constant_dynamic-update-slice_fusion.2
  1.8 0.8 constant_dynamic-update-slice_fusion.1
  2.7 1.0 bitcast_dynamic-update-slice_fusion
  3.6 0.7 constant_dynamic-update-slice_fusion.shard
  4.4 0.0 copy-start
  4.4 0.8 copy-done
  5.2 92.4 %gather_rows.1 = bf16[32,64,5248]{2,1,0:T(8,128)(2,1)} custom-call(bf16[64,5248]{1,0:T(8,128)(2,1)} %copy-done), custom_call_target="tpu_custom_call" | custom-call | tf_op jit(solution)/shard_map/gather_rows/pallas_call | solution.py:177
  97.7 0.0 copy-start.1
  97.7 1.2 slice_convert_fusion
  98.9 0.3 copy.26
  99.2 0.0 copy-done.1
  99.2 0.3 fusion.15
  99.5 2.6 %fusion.18 = f32[256,512]{0,1:T(8,128)S(1)} fusion(bf16[2048,5248]{1,0:T(8,128)(2,1)} %bitcast.33, bf16[256,2048]{1,0:T(8,128)(2,1)S(1)} %copy-done.1, f32[2048]{0:T(1024)S(1)} %bitcast.42, f32[256]{0:T(256)S(1)} %add_rsqrt_fusion), kind=kOutput, calls=%fused_computation.20 | convolution fusion | flops 538968064 | bytes 3679232 | tf_op jit(solution)/shard_map/dot_general | solution.py:223
  102.2 7.0 %fusion.3 = f32[256,2048]{0,1:T(8,128)S(1)} fusion(bf16[2048,5248]{1,0:T(8,128)(2,1)} %bitcast.34, bf16[256,2048]{1,0:T(8,128)(2,1)S(1)} %copy-done.1, f32[2048]{0:T(1024)S(1)} %bitcast.43, f32[256]{0:T(256)S(1)} %add_rsqrt_fusion), kind=kOutput, calls=%fused_computation.3 | convolution fusion | flops 2149580800 | bytes 11543552 | tf_op jit(solution)/shard_map/dot_general | solution.py:222
  109.2 0.2 slice_negate_fusion
  109.4 0.2 fusion.39
  109.6 1.3 %fusion.28 = f32[8,256,256,4]{2,1,3,0:T(8,128)S(1)} fusion(f32[256,8,4,32]{0,3,2,1:T(8,128)S(1)} %get-tuple-element.6, f32[256,8,4,32]{0,3,2,1:T(8,128)S(1)} %get-tuple-element.5, f32[256,8,4,64]{0,3,2,1:T(8,128)S(1)} %bitcast.38, f32[256,64]{0,1:T(8,128)S(1)} %get-tuple-element.14, f32[256,64]{0,1:T(8,128)S(1)} %get-tuple-element.13, ...), kind=kOutput, calls=%fused_computation.29 | convolution fusion | flops 271712256 | bytes 13762560 | tf_op jit(solution)/shard_map/qkgd,skd->kgqs/dot_general | solution.py:233
  111.0 4.6 %fusion.46 = (f32[8,4,256]{2,1,0:T(4,128)S(1)}, f32[8,4,256,256]{2,3,1,0:T(8,128)}) fusion(f32[8,256,256,4]{2,1,3,0:T(8,128)S(1)} %fusion.28, pred[256,256]{0,1:T(8,128)(4,1)S(1)} %iota_compare_fusion), kind=kOutput, calls=%fused_computation.57 | output fusion | flops 12583167 | bytes 16875520 | tf_op jit(solution)/shard_map/sub | solution.py:239
  115.6 2.3 %fusion.25 = bf16[256,512]{1,0:T(8,128)(2,1)S(1)} fusion(bf16[2048,5248]{1,0:T(8,128)(2,1)} %bitcast.35, bf16[256,2048]{1,0:T(8,128)(2,1)S(1)} %copy-done.1, f32[2048]{0:T(1024)S(1)} %bitcast.44, f32[256]{0:T(256)S(1)} %add_rsqrt_fusion), kind=kOutput, calls=%fused_computation.28 | convolution fusion | flops 539099136 | bytes 3417088 | tf_op jit(solution)/shard_map/dot_general | solution.py:224
  117.9 0.1 copy.16
  118.0 4.3 %fusion.24 = bf16[8,64,4,256]{3,1,2,0:T(8,128)(2,1)S(1)} fusion(bf16[256,8,64,1]{0,2,3,1:T(8,128)(2,1)S(1)} %bitcast.41, f32[8,4,256,256]{2,3,1,0:T(8,128)} %get-tuple-element.12, f32[8,4,256]{2,1,0:T(4,128)S(1)} %get-tuple-element.11), kind=kOutput, calls=%fused_computation.27 | convolution fusion | flops 273154048 | bytes 9732096 | tf_op jit(solution)/shard_map/kgqs,skd->qkgd/dot_general | solution.py:241
  122.3 6.8 %fusion.12 = bf16[256,2048]{1,0:T(8,128)(2,1)} fusion(bf16[256,2048]{0,1:T(8,128)(2,1)S(1)} %bitcast.45, bf16[2048,5248]{1,0:T(8,128)(2,1)} %bitcast.36, bf16[256,2048]{1,0:T(8,128)(2,1)S(1)} %copy-done.1), kind=kOutput, calls=%fused_computation.16 | convolution fusion | flops 2149056512 | bytes 11534336 | tf_op jit(solution)/shard_map/dot_general | solution.py:243
  (5 shorter events, 0.1 us)
Async XLA Ops:
  4.4 0.8 copy-start
  97.7 1.5 %copy-start.1 = (bf16[256,2048]{1,0:T(8,128)(2,1)S(1)}, bf16[256,2048]{1,0:T(8,128)(2,1)}, u32[]{:S(2)}) copy-start(bf16[256,2048]{1,0:T(8,128)(2,1)} %param.6) | copy-start | bytes 3145732
